TPU v7x, 32 devices: a whole 2x2x4 slice. The times are simulated.
32 devices in a mesh: ep: 4 (over y, core), etp: 8 (over z, x).
Axes of the slice: x: 2, y: 2, z: 4, core: 2. Of those that a mesh axis runs over, the one named last changes fastest.
Arguments:
- tokens: bfloat16 [4096, 7168], P(('ep', 'etp')), may hold values from -6 to 6
- expert_ids: int32 [4096, 8], P(('ep', 'etp')), may hold values from 0 to 383, all different within a row; in each aligned block of 128 rows (0 to 127, 128 to 255, ...) at most 3 rows name the same one
- gate_q: int32 [4096, 8], P(('ep', 'etp')), may hold values from 1 to 1024
- w_gate: bfloat16 [4, 7168, 2048], P('ep', None, 'etp'), may hold values from -0.0625 to 0.0625
- w_up: bfloat16 [4, 7168, 2048], P('ep', None, 'etp'), may hold values from -0.0625 to 0.0625
- w_down: bfloat16 [4, 2048, 7168], P('ep', 'etp'), may hold values from -0.125 to 0.125
Outputs:
- mixed: bfloat16 [4096, 7168], P(('ep', 'etp'))
Inputs may be any that keep to these rules, and one draw needn't show every extreme that they name: `expert_ids`: each row names 8 different experts; among the 128 rows of one device no expert is named by more than 3 rows.
All inputs are finite; a program needn't handle non-finite values.
Results may differ from a plain program's by a relative error of at most 0.014.
Values may be sent and summed in bfloat16 or wider, within the bound.
A program may use at most 64 MiB of HBM per device.

v0:
```python
import jax
import jax.numpy as jnp
from jax import lax
from jax.sharding import PartitionSpec as P

CAP = 3


def body(tokens, expert_ids, gate_q, w_gate, w_up, w_down):
    groups = lax.axis_size("ep")
    members = lax.axis_size("etp")
    capacity = CAP
    width = tokens.shape[1]
    count_rows = tokens.shape[0]
    flat_ids = expert_ids.reshape(-1)
    owner_hot = (flat_ids[:, None] == jnp.arange(groups, dtype=jnp.int32)[None, :]).astype(
        jnp.int32
    )
    earlier = jnp.cumsum(owner_hot, axis=0) - owner_hot
    position = jnp.sum(earlier * owner_hot, axis=1)
    column = jnp.where(flat_ids < groups, flat_ids * capacity + position, -1)
    select = (column[:, None] == jnp.arange(groups * capacity, dtype=jnp.int32)[None, :]).astype(
        jnp.float32
    )
    select = select.reshape(count_rows, -1, groups * capacity)
    placing = jnp.sum(select, axis=1)
    gate_scale = gate_q.astype(jnp.float32) / 1024.0
    scaling = jnp.sum(select * gate_scale[:, :, None], axis=1)
    bucket = jnp.einsum(
        "tc,td->cd", placing.astype(jnp.bfloat16), tokens, preferred_element_type=jnp.float32
    )
    bucket = bucket.astype(jnp.bfloat16).reshape(groups, capacity, width)
    gathered = lax.all_gather(bucket, "etp", axis=1, tiled=True)
    arrived = lax.all_to_all(gathered, "ep", split_axis=0, concat_axis=0, tiled=True)
    gate = jnp.dot(arrived, w_gate[0], preferred_element_type=jnp.float32)
    upper = jnp.dot(arrived, w_up[0], preferred_element_type=jnp.float32)
    hidden = (jax.nn.silu(gate) * upper).astype(jnp.bfloat16)
    inner = hidden.shape[2]
    ordered = (
        hidden.reshape(groups, members, capacity, inner).transpose(1, 0, 2, 3).reshape(-1, inner)
    )
    term = jnp.dot(ordered, w_down[0], preferred_element_type=jnp.float32)
    rounded = lax.optimization_barrier(term.astype(jnp.bfloat16))
    summed = lax.psum_scatter(
        rounded.astype(jnp.float32).astype(jnp.bfloat16), "etp", scatter_dimension=0, tiled=True
    )
    local_out = summed.reshape(groups, capacity, width)
    results = lax.all_to_all(local_out, "ep", split_axis=0, concat_axis=0, tiled=True)
    flat_out = results.reshape(groups * capacity, width).astype(jnp.float32)
    mixed = jnp.dot(scaling, flat_out, precision=lax.Precision.HIGHEST)
    return mixed.astype(jnp.bfloat16)


def solution(mesh):
    in_specs = (
        P(("ep", "etp"), None),
        P(("ep", "etp"), None),
        P(("ep", "etp"), None),
        P("ep", None, "etp"),
        P("ep", None, "etp"),
        P("ep", "etp", None),
    )
    out_specs = P(("ep", "etp"), None)
    return jax.shard_map(body, mesh=mesh, in_specs=in_specs, out_specs=out_specs, check_vma=False)
```

profile of v0, /device:TPU:0, one launch (start us, length us, event | category | flops | bytes accessed | tf_op | source)
XLA Modules:
  0.0 157.0 jit_solution(10917868213449177721)
XLA Ops:
  6.5 0.0 copy-start
  6.5 0.0 all-gather.2.cloned.1.call-start
  6.5 0.9 copy.40
  7.5 0.1 eq.43
  7.6 0.1 eq.39
  7.7 1.1 reduce-window.6
  8.8 0.2 slice_reduce_fusion
  9.0 0.2 reduce-window.9
  9.2 0.1 add_bitcast_fusion
  9.3 0.1 reduce_sum.30
  9.4 0.7 add_select_fusion
  10.2 0.7 convert_multiply_fusion
  10.9 0.0 copy-done
  10.9 0.3 convolution_convert_fusion.2
  11.2 0.1 reshape.56
  11.4 0.8 copy.43
  12.2 0.0 all-gather.2.cloned.1.call-update
  12.2 45.0 %all-gather.2.cloned.1.call-done = bf16[4,24,7168]{2,0,1:T(4,128)(2,1)} async-done(((bf16[4,3,7168]{2,0,1:T(4,128)(2,1)}), bf16[4,24,7168]{2,0,1:T(4,128)(2,1)}) %all-gather.2.cloned.1.call-update) | async-done | bytes 1376272 | tf_op jit(solution)/shard_map/all_gather | solution.py:33
  57.2 0.0 copy-start.1
  57.2 1.9 %copy.44 = bf16[4,24,7168]{2,1,0:T(8,128)(2,1)S(1)} copy(bf16[4,24,7168]{2,0,1:T(4,128)(2,1)} %all-gather.2.cloned.1.call-done) | data formatting | bytes 2752512 | tf_op jit(solution)/shard_map/all_gather | solution.py:33
  59.1 20.5 %all_to_all.10 = bf16[4,24,7168]{2,1,0:T(8,128)(2,1)S(1)} all-to-all(bf16[4,24,7168]{2,1,0:T(8,128)(2,1)S(1)} %copy.44), channel_id=1, replica_groups=mesh['ep'=4,'etp'=8] {'ep'}, dimensions={0} | all-to-all | bytes 2752512 | tf_op jit(solution)/shard_map/all_to_all | solution.py:34
  79.6 0.0 copy-done.1
  79.6 0.0 copy-start.2
  79.6 0.7 fusion.4
  80.3 1.3 copy-done.2
  81.6 0.7 fusion.9
  82.5 2.8 %convolution_convert_fusion.1 = bf16[96,7168]{1,0:T(8,128)(2,1)S(1)} fusion(bf16[96,256]{1,0:T(8,128)(2,1)S(1)} %reshape.58, bf16[1,256,7168]{2,1,0:T(8,128)(2,1)} %param.11), kind=kOutput, calls=%fused_computation.1 | convolution fusion | flops 353009664 | bytes 5095424 | tf_op jit(solution)/shard_map/dot_general | solution.py:42
  85.2 0.0 copy-start.3
  85.3 43.2 %fusion = bf16[16,7168]{1,0:T(8,128)(2,1)S(1)} fusion(bf16[96,7168]{1,0:T(8,128)(2,1)S(1)} %convolution_convert_fusion.1), kind=kCustom, calls=%all-reduce-scatter | all-reduce-scatter fusion | flops 917505 | bytes 1606144
  128.5 1.5 collective-permute-start
  130.1 0.1 slice.9
  130.1 4.1 %collective-permute-start.1 = (bf16[12,7168]{1,0:T(8,128)(2,1)S(1)}, bf16[12,7168]{1,0:T(8,128)(2,1)S(1)}, u32[]{:S(2)}, u32[]{:S(2)}) collective-permute-start(bf16[12,7168]{1,0:T(8,128)(2,1)S(1)} %slice.9), channel_id=1, source_target_pairs={{0,2},{1,3},{2,4},{3,5},{4,6},{5,7},{8,10},{9,11},{10,12},{11,13},... | collective-permute-start | bytes 516104
  134.2 0.0 copy-done.3
  134.2 0.6 dynamic-slice.4
  135.4 2.3 %collective-permute-done.1 = bf16[12,7168]{1,0:T(8,128)(2,1)S(1)} collective-permute-done((bf16[12,7168]{1,0:T(8,128)(2,1)S(1)}, bf16[12,7168]{1,0:T(8,128)(2,1)S(1)}, u32[]{:S(2)}, u32[]{:S(2)}) %collective-permute-start.1) | collective-permute-done | bytes 172064
  137.7 0.0 collective-permute-done
  137.7 1.2 concatenate
  138.9 0.1 constant_dynamic-slice_fusion
  139.0 0.1 reshape.59
  139.1 8.0 %all_to_all.11 = bf16[4,3,7168]{2,1,0:T(4,128)(2,1)S(1)} all-to-all(bf16[4,3,7168]{2,1,0:T(4,128)(2,1)S(1)} %reshape.59), channel_id=1, replica_groups=mesh['ep'=4,'etp'=8] {'ep'}, dimensions={0} | all-to-all | bytes 344064 | tf_op jit(solution)/shard_map/all_to_all | solution.py:48
  147.1 0.2 reshape.60
  147.3 2.9 %convolution_convert_fusion = bf16[128,7168]{1,0:T(8,128)(2,1)} fusion(f32[128,12]{0,1:T(8,128)S(1)} %get-tuple-element.6, bf16[12,7168]{1,0:T(8,128)(2,1)S(1)} %reshape.60), kind=kOutput, calls=%fused_computation | convolution fusion | flops 133038080 | bytes 2013184 | tf_op jit(solution)/shard_map/dot_general | solution.py:50
  (7 shorter events, 0.2 us)
Async XLA Ops:
  6.5 4.4 %copy-start = (bf16[128,7168]{1,0:T(8,128)(2,1)S(1)}, bf16[128,7168]{1,0:T(8,128)(2,1)}, u32[]{:S(2)}) copy-start(bf16[128,7168]{1,0:T(8,128)(2,1)} %param.6) | copy-start | bytes 5505028
  6.5 50.7 %all-gather.2.cloned.1.call-start = ((), (), s32[]{:S(2)}) async-start(), calls=%async_computation.2 | async-start | bytes 1548288 | tf_op jit(solution)/shard_map/all_gather | solution.py:33
  57.2 22.4 %copy-start.1 = (bf16[1,7168,256]{2,1,0:T(8,128)(2,1)S(1)}, bf16[1,7168,256]{2,1,0:T(8,128)(2,1)}, u32[]{:S(2)}) copy-start(bf16[1,7168,256]{2,1,0:T(8,128)(2,1)} %param.9) | copy-start | bytes 11010052
  79.6 2.0 %copy-start.2 = (bf16[1,7168,256]{2,1,0:T(8,128)(2,1)S(1)}, bf16[1,7168,256]{2,1,0:T(8,128)(2,1)}, u32[]{:S(2)}) copy-start(bf16[1,7168,256]{2,1,0:T(8,128)(2,1)} %param.10) | copy-start | bytes 11010052
  85.2 48.9 %copy-start.3 = (u32[32]{0:T(128)S(1)}, u32[32]{0:T(128)}, u32[]{:S(2)}) copy-start(u32[32]{0:T(128)} %constant.26) | copy-start | bytes 388
  128.5 9.2 %collective-permute-start = (bf16[16,7168]{1,0:T(8,128)(2,1)S(1)}, bf16[16,7168]{1,0:T(8,128)(2,1)S(1)}, u32[]{:S(2)}, u32[]{:S(2)}) collective-permute-start(bf16[16,7168]{1,0:T(8,128)(2,1)S(1)} %fusion), channel_id=1, source_target_pairs={{0,1},{1,2},{2,3},{3,4},{4,5},{5,6},{6,7},{8,9},{9,10},{10,11},{11... | collective-permute-start | bytes 688136
  130.1 7.6 %collective-permute-start.1 = (bf16[12,7168]{1,0:T(8,128)(2,1)S(1)}, bf16[12,7168]{1,0:T(8,128)(2,1)S(1)}, u32[]{:S(2)}, u32[]{:S(2)}) collective-permute-start(bf16[12,7168]{1,0:T(8,128)(2,1)S(1)} %slice.9), channel_id=1, source_target_pairs={{0,2},{1,3},{2,4},{3,5},{4,6},{5,7},{8,10},{9,11},{10,12},{11,13},... | collective-permute-start | bytes 516104
Sparse Core Ops, SparseCore 0:
  12.3 44.8 all-gather.1
where the time goes:
time: 157 us
  blocking collectives  71.8 us (46%)
  waiting for transfers between devices  47.3 us (30%)
  between operations  14.2 us (9%)
  local copies, waits for them, and re-layouts  7.82 us (5%)
  matrix products  7.42 us (5%)
  starting transfers between devices  5.6 us (4%)
  other arithmetic  2.87 us (2%)
    all_gather x1, waiting for transfers between devices, body(): gathered = lax.all_gather(bucket, 'etp', axis=1, tiled=True)  45 us
    unnamed x1, blocking collectives  43.2 us
    all_to_all x1, blocking collectives, body(): lax.all_to_all(gathered, 'ep', split_axis=0, concat_axis=0, tiled=True)  20.5 us
    all_to_all x1, blocking collectives, body(): lax.all_to_all(local_out, 'ep', split_axis=0, concat_axis=0, tiled=True)  8.03 us
    unnamed x2, starting transfers between devices  5.6 us
    unnamed x13, local copies, waits for them, and re-layouts  4.14 us
  transfers between devices with their start and end apart: 3, of which 2 were waited for; matrix products, arithmetic and copies ran while one was open for 0% of the time, Pallas kernels for 0%

commit v1 on v0

v1 whole, which is shorter than its diff:
```python
import functools

import jax
import jax.numpy as jnp
from jax import lax
from jax.experimental import pallas as pl
from jax.experimental.pallas import tpu as pltpu
from jax.sharding import PartitionSpec as P

CAP = 3
PACK = 4
MESH = pl.DeviceIdType.MESH
F32 = jnp.float32
BF16 = jnp.bfloat16


def split_members(members):
    inner = 1
    while (inner * 2) ** 2 <= members and members % (inner * 2) == 0:
        inner *= 2
    return members // inner, inner


def partner(index, step, count):
    if count & (count - 1):
        return lax.rem(index + step, count)
    out, bit = index, 1
    while bit < count:
        if step & bit:
            out = out + bit - 2 * bit * lax.rem(index // bit, 2)
        bit *= 2
    return out


def slots(ids_ref, columns):
    rows, top = ids_ref.shape
    ids = ids_ref[...]
    column = lax.broadcasted_iota(jnp.int32, (rows, columns), 1)
    expert, lane = column // PACK, column % PACK
    match = jnp.zeros((rows, columns), F32)
    for r in range(top):
        match = match + jnp.where(ids[:, r : r + 1] == expert, 1.0, 0.0)
    first = lax.broadcasted_iota(jnp.int32, (rows, rows), 0)
    second = lax.broadcasted_iota(jnp.int32, (rows, rows), 1)
    lower = jnp.where(second < first, 1.0, 0.0).astype(BF16)
    rank = jnp.dot(lower, match.astype(BF16), preferred_element_type=F32)
    return match, rank, lane, expert


def pick(match, rank, lane, k):
    if k is None:
        return jnp.where((rank == lane.astype(F32)) & (lane < CAP), match, 0.0)
    return jnp.where((rank == k) & (lane == CAP), match, 0.0)


def exchange_kernel(
    sizes, ids_ref, tok_ref, wg_hbm, wu_hbm, wd_hbm, out_ref,
    stage, sendp, recvp, gath, part, xin, zout, zin, backp, backin, wg, wu, wd,
    w_sem, a_send, a_recv, zg_send, zg_recv, xg_send, xg_recv,
    xr_send, xr_recv, zr_send, zr_recv, b_send, b_recv,
):
    EP, Z, X = sizes
    R = PACK * EP
    q = tok_ref.shape[1] // PACK
    me = lax.axis_index("ep")
    m = lax.axis_index("etp")
    z, x = m // X, lax.rem(m, X)

    loads = [
        pltpu.make_async_copy(src, dst, w_sem.at[i])
        for i, (src, dst) in enumerate(((wg_hbm, wg), (wu_hbm, wu), (wd_hbm, wd)))
    ]
    for copy in loads:
        copy.start()

    barrier = pltpu.get_barrier_semaphore()
    eps = [partner(me, s, EP) for s in range(EP)]
    zs = [partner(z, s, Z) for s in range(Z)]
    xs = [partner(x, s, X) for s in range(X)]

    def dev(p=None, zi=None, xi=None):
        zi, xi = z if zi is None else zi, x if xi is None else xi
        return (me if p is None else p, zi * X + xi)

    for s in range(1, EP):
        pl.semaphore_signal(barrier, inc=1, device_id=dev(p=eps[s]), device_id_type=MESH)
    for s in range(1, Z):
        pl.semaphore_signal(barrier, inc=1, device_id=dev(zi=zs[s]), device_id_type=MESH)
    for s in range(1, X):
        pl.semaphore_signal(barrier, inc=1, device_id=dev(xi=xs[s]), device_id_type=MESH)

    columns = -(-R // 128) * 128
    match, rank, lane, _ = slots(ids_ref, columns)
    base = jnp.transpose(pick(match, rank, lane, None))[:R].astype(BF16)
    last = tok_ref[:, CAP * q :]
    for k in range(CAP):
        extra = jnp.transpose(pick(match, rank, lane, k))[:R].astype(BF16)
        cut = pl.ds(k * q, q)
        stage[:, cut] = jnp.dot(base, tok_ref[:, cut], preferred_element_type=F32) + jnp.dot(
            extra, last, preferred_element_type=F32
        )
    for e in range(EP):
        sendp[e] = stage[PACK * e : PACK * (e + 1), :].astype(BF16)

    pl.semaphore_wait(barrier, EP + Z + X - 3)

    pending = []

    def remote(src, dst, ssem, rsem, device):
        copy = pltpu.make_async_remote_copy(
            src_ref=src, dst_ref=dst, send_sem=ssem, recv_sem=rsem,
            device_id=device, device_id_type=MESH,
        )
        copy.start()
        pending.append(copy)

    def arrived(ref, ssem, rsem):
        pltpu.make_async_remote_copy(
            src_ref=ref, dst_ref=ref, send_sem=ssem, recv_sem=rsem,
            device_id=dev(p=eps[-1]), device_id_type=MESH,
        ).wait_recv()

    for s in range(1, EP):
        remote(sendp.at[eps[s]], recvp.at[me], a_send.at[s], a_recv.at[me], dev(p=eps[s]))
    recvp[me] = sendp[me]
    for s in range(1, EP):
        arrived(recvp.at[eps[s]], a_send.at[0], a_recv.at[eps[s]])
    for p in range(EP):
        stage[PACK * p : PACK * (p + 1), :] = recvp[p].astype(F32)
    gath[x, z] = stage[...].astype(BF16)

    def pass_on(zi, s0):
        for s in range(1, X):
            remote(
                gath.at[x, zi], gath.at[x, zi], xg_send.at[s0, s], xg_recv.at[x, zi], dev(xi=xs[s])
            )

    for s in range(1, Z):
        remote(gath.at[x, z], gath.at[x, z], zg_send.at[s], zg_recv.at[z], dev(zi=zs[s]))
    pass_on(z, 0)
    for s in range(1, Z):
        arrived(gath.at[x, zs[s]], zg_send.at[0], zg_recv.at[zs[s]])
        pass_on(zs[s], s)
    for copy in loads[:2]:
        copy.wait()
    for s in range(1, X):
        for t in range(Z):
            arrived(gath.at[xs[s], zs[t]], xg_send.at[0, 0], xg_recv.at[xs[s], zs[t]])
    loads[2].wait()

    rows = Z * R
    inner = wg.shape[1]
    hidden = []
    group = X if X * rows <= 128 else 1
    row = lax.broadcasted_iota(jnp.int32, (group * rows, 1), 0) % PACK

    def unpack_dot(a, w):
        total = None
        for k in range(CAP):
            piece = a[:, k * q : (k + 1) * q]
            main = jnp.dot(piece, w[k * q : (k + 1) * q, :], preferred_element_type=F32)
            total = main if total is None else total + main
            tail = jnp.dot(piece, w[CAP * q :, :], preferred_element_type=F32)
            tail = pltpu.roll(tail, group * rows - (CAP - k), 0)
            total = total + jnp.where(row == k, tail, 0.0)
        return total

    def work(g, carry):
        a = gath[pl.ds(g * group, group)].reshape(group * rows, CAP * q)
        gate = unpack_dot(a, wg)
        upper = unpack_dot(a, wu)
        hid = (gate / (1.0 + jnp.exp(-gate)) * upper).astype(BF16)
        for k in range(CAP):
            main = jnp.dot(hid, wd[:, k * q : (k + 1) * q], preferred_element_type=F32)
            tail = jnp.dot(hid, wd[:, CAP * q :], preferred_element_type=F32)
            tail = pltpu.roll(tail, CAP - k, 0)
            both = jnp.where(row == CAP, tail, main)
            part[pl.ds(g * group, group), :, :, k * q : (k + 1) * q] = both.astype(BF16).reshape(
                group, Z, R, q
            )
            if group == X:
                send_x(k)
        return carry

    order = list(range(Z - 1, -1, -1))

    def send_x(k):
        cut = pl.ds(k * q, q)
        for t in order:
            for s in range(1, X):
                remote(
                    part.at[xs[s], zs[t], :, cut], xin.at[x, zs[t], :, cut],
                    xr_send.at[s, t, k], xr_recv.at[x, zs[t], k], dev(xi=xs[s]),
                )

    if group == X:
        work(0, 0)
    else:
        lax.fori_loop(0, X, work, 0)
        for k in range(CAP):
            send_x(k)

    for k in range(CAP):
        cut = pl.ds(k * q, q)
        for t in order:
            total = part[x, zs[t], :, cut].astype(F32)
            for s in range(1, X):
                arrived(
                    xin.at[xs[s], zs[t], :, cut], xr_send.at[0, 0, 0], xr_recv.at[xs[s], zs[t], k]
                )
                total = total + xin[xs[s], zs[t], :, cut].astype(F32)
            if t:
                zout[zs[t], :, cut] = total.astype(BF16)
                remote(
                    zout.at[zs[t], :, cut], zin.at[z, :, cut],
                    zr_send.at[t, k], zr_recv.at[z, k], dev(zi=zs[t]),
                )
            else:
                stage[:, cut] = total
    for k in range(CAP):
        cut = pl.ds(k * q, q)
        total = stage[:, cut]
        for t in range(1, Z):
            arrived(zin.at[zs[t], :, cut], zr_send.at[0, 0], zr_recv.at[zs[t], k])
            total = total + zin[zs[t], :, cut].astype(F32)
        stage[:, cut] = total
        for p in range(EP):
            backp[p, :, cut] = stage[PACK * p : PACK * (p + 1), cut].astype(BF16)
        for s in range(1, EP):
            remote(
                backp.at[eps[s], :, cut], backin.at[me, :, cut],
                b_send.at[s, k], b_recv.at[me, k], dev(p=eps[s]),
            )
        backin[me, :, cut] = backp[me, :, cut]
    for k in range(CAP):
        cut = pl.ds(k * q, q)
        for s in range(1, EP):
            arrived(backin.at[eps[s], :, cut], b_send.at[0, 0], b_recv.at[eps[s], k])
        for p in range(EP):
            stage[PACK * p : PACK * (p + 1), cut] = backin[p, :, cut].astype(F32)
        out_ref[:, cut] = stage[:, cut].astype(BF16)
    for copy in pending:
        copy.wait_send()


def mix_kernel(ids_ref, gate_ref, rows_ref, out_ref):
    R = rows_ref.shape[0]
    q = rows_ref.shape[1] // CAP
    top = ids_ref.shape[1]
    match, rank, lane, expert = slots(ids_ref, R)
    ids, units = ids_ref[...], gate_ref[...]
    coarse = (units // 32) * 32
    hi = jnp.zeros(match.shape, F32)
    lo = jnp.zeros(match.shape, F32)
    for r in range(top):
        here = ids[:, r : r + 1] == expert
        hi = hi + jnp.where(here, coarse[:, r : r + 1].astype(F32), 0.0)
        lo = lo + jnp.where(here, (units - coarse)[:, r : r + 1].astype(F32), 0.0)
    hi, lo = hi / 1024.0, lo / 1024.0

    def weighted(mask, piece):
        return jnp.dot((hi * mask).astype(BF16), piece, preferred_element_type=F32) + jnp.dot(
            (lo * mask).astype(BF16), piece, preferred_element_type=F32
        )

    tail = None
    for k in range(CAP):
        piece = rows_ref[:, k * q : (k + 1) * q]
        out_ref[:, k * q : (k + 1) * q] = weighted(pick(match, rank, lane, None), piece).astype(BF16)
        term = weighted(pick(match, rank, lane, k), piece)
        tail = term if tail is None else tail + term
    out_ref[:, CAP * q :] = tail.astype(BF16)


def body(sizes, tokens, expert_ids, gate_q, w_gate, w_up, w_down):
    EP, Z, X = sizes
    R = PACK * EP
    count, width = tokens.shape
    q = width // PACK
    W = CAP * q
    inner = w_gate.shape[2]
    vmem = pl.BlockSpec(memory_space=pltpu.VMEM)
    hbm = pl.BlockSpec(memory_space=pl.ANY)
    dma = pltpu.SemaphoreType.DMA
    rows = pl.pallas_call(
        functools.partial(exchange_kernel, sizes),
        out_shape=jax.ShapeDtypeStruct((R, W), BF16),
        in_specs=[vmem, vmem, hbm, hbm, hbm],
        out_specs=vmem,
        scratch_shapes=[
            pltpu.VMEM((R, W), F32),
            pltpu.VMEM((EP, PACK, W), BF16),
            pltpu.VMEM((EP, PACK, W), BF16),
            pltpu.VMEM((X, Z, R, W), BF16),
            pltpu.VMEM((X, Z, R, W), BF16),
            pltpu.VMEM((X, Z, R, W), BF16),
            pltpu.VMEM((Z, R, W), BF16),
            pltpu.VMEM((Z, R, W), BF16),
            pltpu.VMEM((EP, PACK, W), BF16),
            pltpu.VMEM((EP, PACK, W), BF16),
            pltpu.VMEM((width, inner), BF16),
            pltpu.VMEM((width, inner), BF16),
            pltpu.VMEM((inner, width), BF16),
            dma((3,)),
            dma((EP,)), dma((EP,)),
            dma((Z,)), dma((Z,)),
            dma((Z, X)), dma((X, Z)),
            dma((X, Z, CAP)), dma((X, Z, CAP)),
            dma((Z, CAP)), dma((Z, CAP)),
            dma((EP, CAP)), dma((EP, CAP)),
        ],
        compiler_params=pltpu.CompilerParams(
            collective_id=0, has_side_effects=True, vmem_limit_bytes=64_000_000
        ),
    )(expert_ids, tokens, w_gate[0], w_up[0], w_down[0])
    return pl.pallas_call(
        mix_kernel,
        out_shape=jax.ShapeDtypeStruct((count, width), BF16),
        in_specs=[vmem, vmem, vmem],
        out_specs=vmem,
    )(expert_ids, gate_q, rows)


def solution(mesh):
    in_specs = (
        P(("ep", "etp"), None),
        P(("ep", "etp"), None),
        P(("ep", "etp"), None),
        P("ep", None, "etp"),
        P("ep", None, "etp"),
        P("ep", "etp", None),
    )
    sizes = (mesh.shape["ep"],) + split_members(mesh.shape["etp"])
    out_specs = P(("ep", "etp"), None)
    return jax.shard_map(
        functools.partial(body, sizes), mesh=mesh, in_specs=in_specs, out_specs=out_specs,
        check_vma=False,
    )
```

time: 157 us -> 64.6 us (0.41)
  blocking collectives: 71.8 us -> 0 us
  Pallas kernels: 0 us -> 61.5 us
  waiting for transfers between devices: 47.3 us -> 0 us
  between operations: 14.2 us -> 0.01 us
  matrix products: 7.42 us -> 0 us
  starting transfers between devices: 5.6 us -> 0 us
  local copies, waits for them, and re-layouts: 7.82 us -> 2.81 us
  other arithmetic: 2.87 us -> 0 us
    pallas_call x0 -> x2, Pallas kernels: none -> 61.5 us  [the longest x1 57.1 us: body(): pl.pallas_call(functools.partial(exchange_kernel, sizes), out_shape=jax.S...]
    all_gather x1 -> x0, waiting for transfers between devices: 45 us -> none  [body(): gathered = lax.all_gather(bucket, 'etp', axis=1, tiled=True)]
    unnamed x1 -> x0, blocking collectives: 43.2 us -> none
    all_to_all x2 -> x0, blocking collectives: 28.5 us -> none  [the longest x1 20.5 us: body(): lax.all_to_all(gathered, 'ep', split_axis=0, concat_axis=0, tiled=True)]
    dot_general x5 -> x0, matrix products: 7.42 us -> none  [the longest x1 2.86 us: body(): mixed = jnp.dot(scaling, flat_out, precision=lax.Precision.HIGHEST)]
    unnamed x2 -> x0, starting transfers between devices: 5.6 us -> none
    unnamed x3 -> x0, waiting for transfers between devices: 2.28 us -> none
    all_gather x1 -> x0, local copies, waits for them, and re-layouts: 1.89 us -> none  [body(): gathered = lax.all_gather(bucket, 'etp', axis=1, tiled=True)]
  transfers between devices with their start and end apart: 3 -> 0, of which waited for: 2 -> 0; matrix products, arithmetic and copies ran while one was open for 0% -> 0% of each run, Pallas kernels for 0% -> 0%
where the time goes in v1:
time: 64.6 us; the launch traced here: 64.4 us
  Pallas kernels  61.5 us (95%)
  local copies, waits for them, and re-layouts  2.81 us (4%)
    pallas_call x1, Pallas kernels, body(): pl.pallas_call(functools.partial(exchange_kernel, sizes), out_shape=jax.S...  57.1 us
    pallas_call x1, Pallas kernels, body(): pl.pallas_call(mix_kernel, out_shape=jax.ShapeDtypeStruct((count, width),...  4.39 us
    unnamed x2, local copies, waits for them, and re-layouts  2.81 us

profile of v1, /device:TPU:0, one launch (start us, length us, event | category | flops | bytes accessed | tf_op | source)
XLA Modules:
  0.0 64.4 jit_solution(5060232522446185930)
XLA Ops:
  0.0 1.4 %copy.8.ids_ref = s32[128,8]{1,0:T(8,128)} copy(s32[128,8]{0,1:T(8,128)} %param.7) | data formatting | bytes 8192 | tf_op args[1]
  1.4 1.4 %copy.9.gate_ref = s32[128,8]{1,0:T(8,128)} copy(s32[128,8]{0,1:T(8,128)} %param.8) | data formatting | bytes 8192 | tf_op args[2]
  2.8 57.1 %shard_map.64.rows_ref = bf16[16,5376]{1,0:T(8,128)(2,1)} custom-call(s32[128,8]{1,0:T(8,128)} %copy.8.ids_ref, bf16[128,7168]{1,0:T(8,128)(2,1)} %tok_ref.1, bf16[7168,256]{1,0:T(8,128)(2,1)} %bitcast.3, bf16[7168,256]{1,0:T(8,128)(2,1)} %bitcast.4, bf16[256,7168]{1,0:T(8,128)(2,1)} %bitcast.5), custom_call_target="tpu_custom_call" | custom-call | tf_op jit(solution)/shard_map/pallas_call | solution.py:285
  60.0 4.4 %shard_map.65 = bf16[128,7168]{1,0:T(8,128)(2,1)} custom-call(s32[128,8]{1,0:T(8,128)} %copy.8.ids_ref, s32[128,8]{1,0:T(8,128)} %copy.9.gate_ref, bf16[16,5376]{1,0:T(8,128)(2,1)} %shard_map.64.rows_ref), custom_call_target="tpu_custom_call" | custom-call | tf_op jit(solution)/shard_map/pallas_call | solution.py:316

commit v2 on v1

v2 whole, which is shorter than its diff:
```python
import functools

import jax
import jax.numpy as jnp
from jax import lax
from jax.experimental import pallas as pl
from jax.experimental.pallas import tpu as pltpu
from jax.sharding import PartitionSpec as P

CAP = 3
PACK = 4
MESH = pl.DeviceIdType.MESH
F32 = jnp.float32
BF16 = jnp.bfloat16


def split_members(members):
    inner = 1
    while (inner * 2) ** 2 <= members and members % (inner * 2) == 0:
        inner *= 2
    return members // inner, inner


def partner(index, step, count):
    if count & (count - 1):
        return lax.rem(index + step, count)
    out, bit = index, 1
    while bit < count:
        if step & bit:
            out = out + bit - 2 * bit * lax.rem(index // bit, 2)
        bit *= 2
    return out


def slots(ids_ref, columns):
    top, rows = ids_ref.shape
    ids = ids_ref[...]
    column = lax.broadcasted_iota(jnp.int32, (columns, rows), 0)
    expert, lane = column // PACK, column % PACK
    match = jnp.zeros((columns, rows), F32)
    for r in range(top):
        match = match + jnp.where(ids[r : r + 1, :] == expert, 1.0, 0.0)
    first = lax.broadcasted_iota(jnp.int32, (rows, rows), 0)
    second = lax.broadcasted_iota(jnp.int32, (rows, rows), 1)
    upper = jnp.where(first < second, 1.0, 0.0).astype(BF16)
    rank = jnp.dot(match.astype(BF16), upper, preferred_element_type=F32)
    return match, rank, lane, expert


def pick(match, rank, lane, k):
    if k is None:
        return jnp.where((rank == lane.astype(F32)) & (lane < CAP), match, 0.0)
    return jnp.where((rank == k) & (lane == CAP), match, 0.0)


def exchange_kernel(
    sizes, ids_ref, gate_ref, tok_hbm, wg_hbm, wu_hbm, wd_hbm, out_ref, mix_ref,
    tok_ref, stage, sendp, recvp, gath, part, xin, zout, zin, backp, backin, wg, wu, wd,
    w_sem, t_sem, a_send, a_recv, zg_send, zg_recv, xg_send, xg_recv,
    xr_send, xr_recv, zr_send, zr_recv, b_send, b_recv,
):
    EP, Z, X = sizes
    R = PACK * EP
    q = tok_ref.shape[1] // PACK
    me = lax.axis_index("ep")
    m = lax.axis_index("etp")
    z, x = m // X, lax.rem(m, X)
    eps = [partner(me, s, EP) for s in range(EP)]
    zs = [partner(z, s, Z) for s in range(Z)]
    xs = [partner(x, s, X) for s in range(X)]
    cuts = [pl.ds(k * q, q) for k in range(PACK)]

    def dev(p=None, zi=None, xi=None):
        zi, xi = z if zi is None else zi, x if xi is None else xi
        return (me if p is None else p, zi * X + xi)

    barrier = pltpu.get_barrier_semaphore()
    for s in range(1, EP):
        pl.semaphore_signal(barrier, inc=1, device_id=dev(p=eps[s]), device_id_type=MESH)
    for s in range(1, Z):
        pl.semaphore_signal(barrier, inc=1, device_id=dev(zi=zs[s]), device_id_type=MESH)
    for s in range(1, X):
        pl.semaphore_signal(barrier, inc=1, device_id=dev(xi=xs[s]), device_id_type=MESH)

    feeds = [
        pltpu.make_async_copy(tok_hbm.at[:, cuts[k]], tok_ref.at[:, cuts[k]], t_sem.at[k])
        for k in range(PACK)
    ]
    loads = [
        pltpu.make_async_copy(src, dst, w_sem.at[i])
        for i, (src, dst) in enumerate(((wg_hbm, wg), (wu_hbm, wu), (wd_hbm, wd)))
    ]
    for copy in feeds[::-1] + loads:
        copy.start()

    pending = []

    def remote(src, dst, ssem, rsem, device):
        copy = pltpu.make_async_remote_copy(
            src_ref=src, dst_ref=dst, send_sem=ssem, recv_sem=rsem,
            device_id=device, device_id_type=MESH,
        )
        copy.start()
        pending.append(copy)

    def arrived(ref, ssem, rsem):
        pltpu.make_async_remote_copy(
            src_ref=ref, dst_ref=ref, send_sem=ssem, recv_sem=rsem,
            device_id=dev(p=eps[-1]), device_id_type=MESH,
        ).wait_recv()

    match, rank, lane, expert = slots(ids_ref, R)
    base = pick(match, rank, lane, None)
    extras = [pick(match, rank, lane, k) for k in range(CAP)]
    feeds[CAP].wait()
    for k in range(CAP - 1, -1, -1):
        cut = cuts[k]
        feeds[k].wait()
        stage[:, cut] = jnp.dot(
            base.astype(BF16), tok_ref[:, cut], preferred_element_type=F32
        ) + jnp.dot(extras[k].astype(BF16), tok_ref[:, cuts[CAP]], preferred_element_type=F32)
        for e in range(EP):
            sendp[e, :, cut] = stage[PACK * e : PACK * (e + 1), cut].astype(BF16)
        if k == CAP - 1:
            pl.semaphore_wait(barrier, EP + Z + X - 3)
        for s in range(1, EP):
            remote(
                sendp.at[eps[s], :, cut], recvp.at[me, :, cut],
                a_send.at[s, k], a_recv.at[me, k], dev(p=eps[s]),
            )
        recvp[me, :, cut] = sendp[me, :, cut]

    def pass_on(zi, s0, k):
        for s in range(1, X):
            remote(
                gath.at[x, zi, :, cuts[k]], gath.at[x, zi, :, cuts[k]],
                xg_send.at[s0, s, k], xg_recv.at[x, zi, k], dev(xi=xs[s]),
            )

    for k in range(CAP - 1, -1, -1):
        cut = cuts[k]
        for s in range(1, EP):
            arrived(recvp.at[eps[s], :, cut], a_send.at[0, 0], a_recv.at[eps[s], k])
        for p in range(EP):
            stage[PACK * p : PACK * (p + 1), cut] = recvp[p, :, cut].astype(F32)
        gath[x, z, :, cut] = stage[:, cut].astype(BF16)
        for s in range(1, Z):
            remote(
                gath.at[x, z, :, cut], gath.at[x, z, :, cut],
                zg_send.at[s, k], zg_recv.at[z, k], dev(zi=zs[s]),
            )
        pass_on(z, 0, k)

    units = gate_ref[...]
    coarse = (units // 32) * 32
    hi = jnp.zeros(match.shape, F32)
    lo = jnp.zeros(match.shape, F32)
    for r in range(ids_ref.shape[0]):
        here = ids_ref[r : r + 1, :] == expert
        hi = hi + jnp.where(here, coarse[r : r + 1, :].astype(F32), 0.0)
        lo = lo + jnp.where(here, (units - coarse)[r : r + 1, :].astype(F32), 0.0)
    hi, lo = hi / 1024.0, lo / 1024.0
    parts = [w * mask for mask in [base] + extras for w in (hi, lo)]
    mix_ref[...] = jnp.transpose(jnp.concatenate(parts, axis=0)).astype(BF16)

    def relay(k):
        for s in range(1, Z):
            arrived(gath.at[x, zs[s], :, cuts[k]], zg_send.at[0, 0], zg_recv.at[zs[s], k])
            pass_on(zs[s], s, k)

    def gathered(k):
        for t in range(Z):
            for s in range(1, X):
                arrived(
                    gath.at[xs[s], zs[t], :, cuts[k]], xg_send.at[0, 0, 0],
                    xg_recv.at[xs[s], zs[t], k],
                )

    group = X if X * Z * R <= 128 else 1
    count = group * Z * R
    row = lax.broadcasted_iota(jnp.int32, (count, 1), 0) % PACK

    def enter(g, k, w, total):
        a = gath[pl.ds(g * group, group), :, :, cuts[k]].reshape(count, q)
        main = jnp.dot(a, w[k * q : (k + 1) * q, :], preferred_element_type=F32)
        tail = jnp.dot(a, w[CAP * q :, :], preferred_element_type=F32)
        tail = pltpu.roll(tail, count - (CAP - k), 0)
        main = main + jnp.where(row == k, tail, 0.0)
        return main if total is None else total + main

    def leave(g, gate, upper):
        hid = (gate / (1.0 + jnp.exp(-gate)) * upper).astype(BF16)
        last = jnp.dot(hid, wd[:, cuts[CAP]], preferred_element_type=F32)
        for k in range(CAP):
            main = jnp.dot(hid, wd[:, cuts[k]], preferred_element_type=F32)
            both = jnp.where(row == CAP, pltpu.roll(last, CAP - k, 0), main)
            part[pl.ds(g * group, group), :, :, cuts[k]] = both.astype(BF16).reshape(
                group, Z, R, q
            )
            if group == X:
                send_x(k)

    order = list(range(Z - 1, -1, -1))

    def send_x(k):
        cut = pl.ds(k * q, q)
        for t in order:
            for s in range(1, X):
                remote(
                    part.at[xs[s], zs[t], :, cut], xin.at[x, zs[t], :, cut],
                    xr_send.at[s, t, k], xr_recv.at[x, zs[t], k], dev(xi=xs[s]),
                )

    def ready():
        for copy in loads:
            copy.wait()

    if group == X:
        gate = upper = None
        for step in range(CAP + 1):
            if step < CAP:
                relay(CAP - 1 - step)
            if step == 1:
                ready()
            if step:
                k = CAP - step
                gathered(k)
                gate = enter(0, k, wg, gate)
                upper = enter(0, k, wu, upper)
        leave(0, gate, upper)
    else:
        for k in range(CAP):
            relay(k)
        for k in range(CAP):
            gathered(k)
        ready()

        def work(g, carry):
            gate = upper = None
            for k in range(CAP):
                gate = enter(g, k, wg, gate)
                upper = enter(g, k, wu, upper)
            leave(g, gate, upper)
            return carry

        lax.fori_loop(0, X, work, 0)
        for k in range(CAP):
            send_x(k)

    for k in range(CAP):
        cut = pl.ds(k * q, q)
        for t in order:
            total = part[x, zs[t], :, cut].astype(F32)
            for s in range(1, X):
                arrived(
                    xin.at[xs[s], zs[t], :, cut], xr_send.at[0, 0, 0], xr_recv.at[xs[s], zs[t], k]
                )
                total = total + xin[xs[s], zs[t], :, cut].astype(F32)
            if t:
                zout[zs[t], :, cut] = total.astype(BF16)
                remote(
                    zout.at[zs[t], :, cut], zin.at[z, :, cut],
                    zr_send.at[t, k], zr_recv.at[z, k], dev(zi=zs[t]),
                )
            else:
                stage[:, cut] = total
    for k in range(CAP):
        cut = pl.ds(k * q, q)
        total = stage[:, cut]
        for t in range(1, Z):
            arrived(zin.at[zs[t], :, cut], zr_send.at[0, 0], zr_recv.at[zs[t], k])
            total = total + zin[zs[t], :, cut].astype(F32)
        stage[:, cut] = total
        for p in range(EP):
            backp[p, :, cut] = stage[PACK * p : PACK * (p + 1), cut].astype(BF16)
        for s in range(1, EP):
            remote(
                backp.at[eps[s], :, cut], backin.at[me, :, cut],
                b_send.at[s, k], b_recv.at[me, k], dev(p=eps[s]),
            )
        backin[me, :, cut] = backp[me, :, cut]
    for k in range(CAP):
        cut = pl.ds(k * q, q)
        for s in range(1, EP):
            arrived(backin.at[eps[s], :, cut], b_send.at[0, 0], b_recv.at[eps[s], k])
        for p in range(EP):
            stage[PACK * p : PACK * (p + 1), cut] = backin[p, :, cut].astype(F32)
        out_ref[:R, cut] = stage[:, cut].astype(BF16)
        out_ref[R:, cut] = stage[:, cut].astype(BF16)
    for copy in pending:
        copy.wait_send()


def mix_kernel(mix_ref, rows_ref, out_hbm, out, sem):
    R2 = rows_ref.shape[0]
    q = rows_ref.shape[1] // CAP
    copies = []
    tail = None

    def emit(k, value):
        cut = pl.ds(k * q, q)
        out[:, cut] = value.astype(BF16)
        copies.append(pltpu.make_async_copy(out.at[:, cut], out_hbm.at[:, cut], sem.at[k]))
        copies[-1].start()

    for k in range(CAP):
        piece = rows_ref[:, k * q : (k + 1) * q]
        emit(k, jnp.dot(mix_ref[:, :R2], piece, preferred_element_type=F32))
        weights = mix_ref[:, (k + 1) * R2 : (k + 2) * R2]
        term = jnp.dot(weights, piece, preferred_element_type=F32)
        tail = term if tail is None else tail + term
    emit(CAP, tail)
    for copy in copies:
        copy.wait()


def body(sizes, tokens, expert_ids, gate_q, w_gate, w_up, w_down):
    EP, Z, X = sizes
    R = PACK * EP
    count, width = tokens.shape
    q = width // PACK
    W = CAP * q
    inner = w_gate.shape[2]
    vmem = pl.BlockSpec(memory_space=pltpu.VMEM)
    hbm = pl.BlockSpec(memory_space=pl.ANY)
    dma = pltpu.SemaphoreType.DMA
    rows, mix = pl.pallas_call(
        functools.partial(exchange_kernel, sizes),
        out_shape=(
            jax.ShapeDtypeStruct((2 * R, W), BF16),
            jax.ShapeDtypeStruct((count, 2 * PACK * R), BF16),
        ),
        in_specs=[vmem, vmem, hbm, hbm, hbm, hbm],
        out_specs=(vmem, vmem),
        scratch_shapes=[
            pltpu.VMEM((count, width), BF16),
            pltpu.VMEM((R, W), F32),
            pltpu.VMEM((EP, PACK, W), BF16),
            pltpu.VMEM((EP, PACK, W), BF16),
            pltpu.VMEM((X, Z, R, W), BF16),
            pltpu.VMEM((X, Z, R, W), BF16),
            pltpu.VMEM((X, Z, R, W), BF16),
            pltpu.VMEM((Z, R, W), BF16),
            pltpu.VMEM((Z, R, W), BF16),
            pltpu.VMEM((EP, PACK, W), BF16),
            pltpu.VMEM((EP, PACK, W), BF16),
            pltpu.VMEM((width, inner), BF16),
            pltpu.VMEM((width, inner), BF16),
            pltpu.VMEM((inner, width), BF16),
            dma((3,)),
            dma((PACK,)),
            dma((EP, CAP)), dma((EP, CAP)),
            dma((Z, CAP)), dma((Z, CAP)),
            dma((Z, X, CAP)), dma((X, Z, CAP)),
            dma((X, Z, CAP)), dma((X, Z, CAP)),
            dma((Z, CAP)), dma((Z, CAP)),
            dma((EP, CAP)), dma((EP, CAP)),
        ],
        compiler_params=pltpu.CompilerParams(
            collective_id=0, has_side_effects=True, vmem_limit_bytes=64_000_000
        ),
    )(expert_ids.T, gate_q.T, tokens, w_gate[0], w_up[0], w_down[0])
    return pl.pallas_call(
        mix_kernel,
        out_shape=jax.ShapeDtypeStruct((count, width), BF16),
        in_specs=[vmem, vmem],
        out_specs=hbm,
        scratch_shapes=[pltpu.VMEM((count, width), BF16), dma((PACK,))],
    )(mix, rows)


def solution(mesh):
    in_specs = (
        P(("ep", "etp"), None),
        P(("ep", "etp"), None),
        P(("ep", "etp"), None),
        P("ep", None, "etp"),
        P("ep", None, "etp"),
        P("ep", "etp", None),
    )
    sizes = (mesh.shape["ep"],) + split_members(mesh.shape["etp"])
    out_specs = P(("ep", "etp"), None)
    return jax.shard_map(
        functools.partial(body, sizes), mesh=mesh, in_specs=in_specs, out_specs=out_specs,
        check_vma=False,
    )
```

time: 64.6 us -> 56.5 us (0.87)
  Pallas kernels: 61.5 us -> 56.3 us
  local copies, waits for them, and re-layouts: 2.81 us -> 0 us
    pallas_call x1, Pallas kernels: 57.1 us -> 53.6 us  [body(): pl.pallas_call(functools.partial(exchange_kernel, sizes), out_shape=(jax....]
    unnamed x2 -> x0, local copies, waits for them, and re-layouts: 2.81 us -> none
    pallas_call x1, Pallas kernels: 4.39 us -> 2.7 us  [body(): pl.pallas_call(mix_kernel, out_shape=jax.ShapeDtypeStruct((count, width),...]
where the time goes in v2:
time: 56.5 us; the launch traced here: 56.3 us
  Pallas kernels  56.3 us (100%)
    pallas_call x1, Pallas kernels, body(): pl.pallas_call(functools.partial(exchange_kernel, sizes), out_shape=(jax....  53.6 us
    pallas_call x1, Pallas kernels, body(): pl.pallas_call(mix_kernel, out_shape=jax.ShapeDtypeStruct((count, width),...  2.7 us

profile of v2, /device:TPU:0, one launch (start us, length us, event | category | flops | bytes accessed | tf_op | source)
XLA Modules:
  0.0 56.3 jit_solution(17917197220778889655)
XLA Ops:
  0.0 53.6 %shard_map.64 = (bf16[32,5376]{1,0:T(8,128)(2,1)}, bf16[128,128]{1,0:T(8,128)(2,1)}) custom-call(s32[8,128]{1,0:T(8,128)} %bitcast.8, s32[8,128]{1,0:T(8,128)} %bitcast.9, bf16[128,7168]{1,0:T(8,128)(2,1)} %tok_hbm.1, bf16[7168,256]{1,0:T(8,128)(2,1)} %bitcast.5, bf16[7168,256]{1,0:T(8,128)(2,1)} %bitcast.6, bf16[256,7168]{1,0:T(8,128)(2,1)} %bitcast.7), custom_call_target="tpu_custom_call" | custom-call | tf_op jit(solution)/shard_map/pallas_call | solution.py:327
  53.6 2.7 %shard_map.65 = bf16[128,7168]{1,0:T(8,128)(2,1)} custom-call(bf16[128,128]{1,0:T(8,128)(2,1)} %get-tuple-element.7.mix_ref, bf16[32,5376]{1,0:T(8,128)(2,1)} %get-tuple-element.8.rows_ref), custom_call_target="tpu_custom_call" | custom-call | tf_op jit(solution)/shard_map/pallas_call | solution.py:363
